TPU v7x, 32 devices: a whole 2x2x4 slice. The times are simulated.
32 devices in a mesh: seq: 8 (over z, core), tp: 4 (over y, x).
Axes of the slice: x: 2, y: 2, z: 4, core: 2. Of those that a mesh axis runs over, the one named last changes fastest.
Arguments:
- hidden_in: bfloat16 [4096, 4608], P('seq'), may hold values from -6 to 6
- pre_gain: float32 [4608], replicated, may hold values from 0.5 to 1.5
- w_query: bfloat16 [4608, 4096], P(None, 'tp'), may hold values from -0.09375 to 0.09375
- key_cache: bfloat16 [8192, 2048], P('seq', 'tp'), may hold values from -12 to 12
- value_cache: bfloat16 [8192, 2048], P('seq', 'tp'), may hold values from -6 to 6
- w_out: bfloat16 [4096, 4608], P('tp'), may hold values from -0.75 to 0.75
- post_gain: float32 [4608], replicated, may hold values from 0.5 to 1.5
- starts: int32 [8], replicated, may hold values from 0 to 7680, as said below
- counts: int32 [8], replicated, may hold values from 512 to 1024, as said below
Outputs:
- layer_out: bfloat16 [4096, 4608], P(('seq', 'tp'))
Inputs may be any that keep to these rules, and one draw needn't show every extreme that they name: The queries of shard s sit at positions starts[s] to starts[s] + 511, all inside the filled rows of shard s, that is from s * 1024 to s * 1024 + counts[s] - 1. `counts`: at least one shard is full.
All inputs are finite; a program needn't handle non-finite values.
Results may differ from a plain program's by a relative error of at most 0.012.
Values may be sent and summed in bfloat16 or wider, within the bound.
A program may use at most 128 MiB of HBM per device.

v0:
```python
import functools
import math

import jax
import jax.numpy as jnp
from jax import lax
from jax.experimental import pallas as pl
from jax.experimental.pallas import tpu as pltpu
from jax.sharding import PartitionSpec as P

HEADS = 32
HD = 128
WINDOW = 4096
NC = 4
QT = 256
NT = 512
SOFT = 50.0
GAIN = SOFT * math.log2(math.e)
MESH = pl.DeviceIdType.MESH
F32 = jnp.float32
BF16 = jnp.bfloat16


def kernel(
    n, n_tp, kvh,
    starts, counts, hidden, pre_gain, wq, key, value, wout, post_gain, out,
    hbuf, wqb, wob, k0, v0, k2, v2, k1, v1, qo, qr, vx, ao, ar, psend, precv,
    proj, rrecv, res, obuf, att,
    hsem, wqsem, wosem, kvsem, ressem, osem,
    s2, r2, s1, r1, sq, rq, sp, rp, ss, rs,
):
    s = lax.axis_index("seq")
    t = lax.axis_index("tp")
    odd = lax.rem(s, 2)
    partner = s + 1 - 2 * odd
    rows, d = hidden.shape
    ctx = key.shape[0]
    sub = rows // (NC * n_tp)
    chunk = rows // NC
    owned = rows // n_tp
    has_prev = s >= 2
    has_next = s + 2 < n

    hcopies = []
    for c in range(NC):
        for b in range(n_tp):
            cp = pltpu.make_async_copy(
                hidden.at[pl.ds(b * owned + c * sub, sub)], hbuf.at[c, b], hsem.at[c, b])
            cp.start()
            hcopies.append(cp)

    def wq_copy(h):
        return pltpu.make_async_copy(
            wq.at[:, pl.ds(pl.multiple_of(h * 2 * HD, 2 * HD), 2 * HD)], wqb.at[h], wqsem.at[h])

    for h in range(kvh):
        wq_copy(h).start()

    barrier = pltpu.get_barrier_semaphore()
    pl.semaphore_signal(barrier, inc=1, device_id=(partner, t), device_id_type=MESH)
    for k in range(1, n_tp):
        pl.semaphore_signal(barrier, inc=1, device_id=(s, lax.rem(t + k, n_tp)), device_id_type=MESH)

    @pl.when(has_prev)
    def _():
        pl.semaphore_signal(barrier, inc=1, device_id=(s - 2, t), device_id_type=MESH)

    @pl.when(has_next)
    def _():
        pl.semaphore_signal(barrier, inc=1, device_id=(s + 2, t), device_id_type=MESH)

    pl.semaphore_wait(
        barrier, n_tp + jnp.where(has_prev, 1, 0) + jnp.where(has_next, 1, 0))

    def cols(h):
        return pl.ds(pl.multiple_of(h * HD, HD), HD)

    def kv_next(h):
        return [
            pltpu.make_async_remote_copy(
                src.at[:, cols(h)], dst.at[h], s2.at[h, j], r2.at[h, j],
                device_id=(s + 2, t), device_id_type=MESH)
            for j, (src, dst) in enumerate(((key, k2), (value, v2)))
        ]

    def kv_own_partner(h):
        return [
            pltpu.make_async_remote_copy(
                src.at[:, cols(h)], dst.at[h], s1.at[h, j], r1.at[h, j],
                device_id=(partner, t), device_id_type=MESH)
            for j, (src, dst) in enumerate(((key, k1), (value, v1)))
        ]

    def kv_relay(h):
        return [
            pltpu.make_async_remote_copy(
                src.at[h], dst.at[h], s1.at[h, j], r1.at[h, j],
                device_id=(partner, t), device_id_type=MESH)
            for j, (src, dst) in enumerate(((k2, k1), (v2, v1)))
        ]

    def q_back(h):
        return pltpu.make_async_remote_copy(
            qo.at[h], qr.at[h], sq.at[h], rq.at[h], device_id=(s - 2, t), device_id_type=MESH)

    def part_next(c):
        return pltpu.make_async_remote_copy(
            psend.at[c], precv.at[c], sp.at[c], rp.at[c],
            device_id=(s + 2, t), device_id_type=MESH)

    def scatter(c, k):
        to = lax.rem(t + k, n_tp)
        return pltpu.make_async_remote_copy(
            proj.at[c, to], rrecv.at[c, k - 1], ss.at[c, k - 1], rs.at[c, k - 1],
            device_id=(s, to), device_id_type=MESH)

    @pl.when(has_next)
    def _():
        for h in range(kvh):
            for cp in kv_next(h):
                cp.start()

    @pl.when(odd == 0)
    def _():
        for h in range(kvh):
            for cp in kv_own_partner(h):
                cp.start()

    def kv_local(h):
        return [
            pltpu.make_async_copy(src.at[:, cols(h)], dst.at[h], kvsem.at[h, j])
            for j, (src, dst) in enumerate(((key, k0), (value, v0)))
        ]

    for h in range(kvh):
        for cp in kv_local(h):
            cp.start()
    wo_copy = pltpu.make_async_copy(wout, wob, wosem)
    wo_copy.start()
    res_copy = pltpu.make_async_copy(
        hidden.at[pl.ds(pl.multiple_of(t * owned, owned), owned)], res, ressem)
    res_copy.start()

    for cp in hcopies:
        cp.wait()

    def norm(i, carry):
        c = i // n_tp
        b = i % n_tp
        x = hbuf[c, b].astype(F32)
        y = x * lax.rsqrt(jnp.mean(x * x, axis=-1, keepdims=True) + 0.1) * pre_gain[...]
        hbuf[c, b] = y.astype(BF16)
        return carry

    lax.fori_loop(0, NC * n_tp, norm, 0)

    def project(h, carry):
        wq_copy(h).wait()
        x = hbuf[...].reshape(rows, d)
        y = jnp.dot(x, wqb[h], preferred_element_type=F32) * ((d // HEADS) ** -0.5 / SOFT)
        y = y.astype(BF16)
        qo[h, 0:rows] = y[:, :HD]
        qo[h, rows:2 * rows] = y[:, HD:]

        @pl.when(has_prev)
        def _():
            q_back(h).start()

        return carry

    lax.fori_loop(0, kvh, project, 0)

    def extend(v, h, filled):
        r = lax.broadcasted_iota(jnp.int32, (ctx, HD), 0)
        ok = r < filled
        vx[:, 0:HD] = jnp.where(ok, v[h].astype(F32), 0.0).astype(BF16)
        vx[:, HD:] = jnp.where(ok, 1.0, 0.0).astype(BF16)

    def unit(q, k, h, acc, first, mode, offset):
        per = QT // chunk

        def tile(i, carry):
            span = pl.ds(pl.multiple_of(i * QT, QT), QT)
            qt = q[h, span]
            ps = []
            kb = 256
            if mode:
                shape = (per, n_tp, sub, kb)
                c0 = lax.rem(i * per, NC)
                pos = (
                    (c0 + lax.broadcasted_iota(jnp.int32, shape, 0)) * sub
                    + lax.broadcasted_iota(jnp.int32, shape, 1) * owned
                    + lax.broadcasted_iota(jnp.int32, shape, 2)
                )
                rel = (lax.broadcasted_iota(jnp.int32, shape, 3) - pos - offset).reshape(QT, kb)
            for b in range(ctx // kb):
                sc = lax.dot_general(
                    qt, k[h, b * kb:(b + 1) * kb], (((1,), (1,)), ((), ())),
                    preferred_element_type=F32)
                p = jnp.exp2(jnp.tanh(sc) * GAIN)
                if mode == 1:
                    p = jnp.where(rel <= -b * kb, p, 0.0)
                elif mode == 2:
                    p = jnp.where(rel > -b * kb, p, 0.0)
                ps.append(p.astype(BF16))
            a = jnp.dot(jnp.concatenate(ps, axis=1), vx[...], preferred_element_type=F32)
            if first:
                acc[h, span] = a
            else:
                acc[h, span] += a
            return carry

        lax.fori_loop(0, 2 * rows // QT, tile, 0, unroll=2)

    off_own = starts[s] - s * ctx
    s_next = jnp.minimum(s + 2, n - 1)
    off_next = starts[s_next] - s_next * ctx + (2 + 2) * ctx - WINDOW
    fill1 = counts[jnp.maximum(s - 1, 0)]
    fill2 = counts[jnp.maximum(s - 2, 0)]

    def own(h, carry):
        for cp in kv_local(h):
            cp.wait()
        extend(v0, h, ctx)
        unit(qo, k0, h, ao, True, 1, off_own)
        ar[h] = jnp.zeros_like(ar[h])
        return carry

    lax.fori_loop(0, kvh, own, 0)

    def far(h, carry):
        @pl.when(has_prev)
        def _():
            for cp in kv_next(h):
                cp.wait_recv()

        @pl.when(has_prev & (odd == 1))
        def _():
            for cp in kv_relay(h):
                cp.start()

        @pl.when(has_next)
        def _():
            q_back(h).wait_recv()

        @pl.when(has_prev)
        def _():
            extend(v2, h, fill2)
            unit(qo, k2, h, ao, False, 0, 0)

            @pl.when(has_next)
            def _():
                unit(qr, k2, h, ar, False, 2, off_next)

        @pl.when(s >= 1)
        def _():
            @pl.when(has_prev | (odd == 1))
            def _():
                for cp in kv_own_partner(h):
                    cp.wait_recv()

            extend(v1, h, fill1)
            unit(qo, k1, h, ao, False, 0, 0)

            @pl.when(has_next)
            def _():
                unit(qr, k1, h, ar, False, 0, 0)

        return carry

    lax.fori_loop(0, kvh, far, 0)

    lane = lax.broadcasted_iota(jnp.int32, (chunk, HD), 1)
    heads = 2 * kvh

    @pl.when(has_next)
    def _():
        for c in range(NC):
            pack = jnp.zeros((chunk, HD), F32)
            for h in range(kvh):
                for g in range(2):
                    r0 = g * rows + c * chunk
                    j = 2 * h + g
                    psend[c, j] = ar[h, r0:r0 + chunk, 0:HD].astype(BF16)
                    den = ar[h, r0:r0 + chunk, HD:2 * HD]
                    hi = den.astype(BF16).astype(F32)
                    pack = jnp.where(lane == j, hi, pack)
                    pack = jnp.where(lane == heads + j, den - hi, pack)
            psend[c, heads] = pack.astype(BF16)
            part_next(c).start()

    wo_copy.wait()

    @pl.when(s < 2)
    def _():
        precv[...] = jnp.zeros_like(precv)

    def finish(c, carry):
        @pl.when(has_prev)
        def _():
            part_next(c).wait_recv()

        pack = precv[c, heads].astype(F32)
        for h in range(kvh):
            for g in range(2):
                j = 2 * h + g
                span = pl.ds(pl.multiple_of(g * rows + c * chunk, chunk), chunk)
                den = (
                    ao[h, span, HD:2 * HD]
                    + pack[:, j:j + 1] + pack[:, heads + j:heads + j + 1]
                )
                num = ao[h, span, 0:HD] + precv[c, j].astype(F32)
                att[:, j * HD:(j + 1) * HD] = (num / den).astype(BF16)

        def column(i, inner):
            cs = pl.ds(pl.multiple_of(i * NT, NT), NT)
            y = jnp.dot(att[...], wob[:, cs], preferred_element_type=F32).astype(BF16)
            proj[c, :, :, cs] = y.reshape(n_tp, sub, NT)
            return inner

        lax.fori_loop(0, d // NT, column, 0)
        for k in range(1, n_tp):
            scatter(c, k).start()
        return carry

    lax.fori_loop(0, NC, finish, 0)
    res_copy.wait()

    def out_copy(c):
        return pltpu.make_async_copy(
            obuf.at[c], out.at[pl.ds(pl.multiple_of(c * sub, sub), sub)], osem.at[c])

    def close(c, carry):
        total = proj[c, t].astype(F32)
        for k in range(1, n_tp):
            scatter(c, k).wait_recv()
            total += rrecv[c, k - 1].astype(F32)
        scale = lax.rsqrt(jnp.mean(total * total, axis=-1, keepdims=True) + 0.1)
        r = res[pl.ds(pl.multiple_of(c * sub, sub), sub)].astype(F32)
        obuf[c] = (r + total * scale * post_gain[...]).astype(BF16)
        out_copy(c).start()
        return carry

    lax.fori_loop(0, NC, close, 0)

    def drain(h, carry):
        @pl.when(has_next)
        def _():
            for cp in kv_next(h):
                cp.wait_send()

        @pl.when(odd == 0)
        def _():
            for cp in kv_own_partner(h):
                cp.wait_send()

        @pl.when(has_prev & (odd == 1))
        def _():
            for cp in kv_relay(h):
                cp.wait_send()

        @pl.when(has_prev)
        def _():
            q_back(h).wait_send()

        return carry

    lax.fori_loop(0, kvh, drain, 0)

    def drain_chunks(c, carry):
        @pl.when(has_next)
        def _():
            part_next(c).wait_send()

        for k in range(1, n_tp):
            scatter(c, k).wait_send()
        out_copy(c).wait()
        return carry

    lax.fori_loop(0, NC, drain_chunks, 0)


def shards(n, n_tp, hidden_in, pre_gain, w_query, key_cache, value_cache, w_out, post_gain, starts, counts):
    rows, d = hidden_in.shape
    ctx, kvw = key_cache.shape
    kvh = kvw // HD
    sub = rows // (NC * n_tp)
    chunk = rows // NC
    dma = pltpu.SemaphoreType.DMA
    kv = pltpu.VMEM((kvh, ctx, HD), BF16)
    any_spec = pl.BlockSpec(memory_space=pl.ANY)
    vmem_spec = pl.BlockSpec(memory_space=pltpu.VMEM)
    smem_spec = pl.BlockSpec(memory_space=pltpu.SMEM)
    return pl.pallas_call(
        functools.partial(kernel, n, n_tp, kvh),
        out_shape=jax.ShapeDtypeStruct((rows // n_tp, d), BF16),
        in_specs=[smem_spec, smem_spec, any_spec, vmem_spec] + [any_spec] * 4 + [vmem_spec],
        out_specs=any_spec,
        scratch_shapes=[
            pltpu.VMEM((NC, n_tp, sub, d), BF16),
            pltpu.VMEM((kvh, d, 2 * HD), BF16),
            pltpu.VMEM(w_out.shape, BF16),
            kv, kv, kv, kv, kv, kv,
            pltpu.VMEM((kvh, 2 * rows, HD), BF16),
            pltpu.VMEM((kvh, 2 * rows, HD), BF16),
            pltpu.VMEM((ctx, 2 * HD), BF16),
            pltpu.VMEM((kvh, 2 * rows, 2 * HD), F32),
            pltpu.VMEM((kvh, 2 * rows, 2 * HD), F32),
            pltpu.VMEM((NC, 2 * kvh + 1, chunk, HD), BF16),
            pltpu.VMEM((NC, 2 * kvh + 1, chunk, HD), BF16),
            pltpu.VMEM((NC, n_tp, sub, d), BF16),
            pltpu.VMEM((NC, n_tp - 1, sub, d), BF16),
            pltpu.VMEM((rows // n_tp, d), BF16),
            pltpu.VMEM((NC, sub, d), BF16),
            pltpu.VMEM((chunk, w_out.shape[0]), BF16),
            dma((NC, n_tp)), dma((kvh,)), dma, dma((kvh, 2)), dma, dma((NC,)),
            dma((kvh, 2)), dma((kvh, 2)), dma((kvh, 2)), dma((kvh, 2)),
            dma((kvh,)), dma((kvh,)), dma((NC,)), dma((NC,)),
            dma((NC, n_tp - 1)), dma((NC, n_tp - 1)),
        ],
        compiler_params=pltpu.CompilerParams(
            collective_id=0, has_side_effects=True, vmem_limit_bytes=67_000_000),
        name="attention_block",
    )(starts, counts, hidden_in, pre_gain.reshape(1, d), w_query, key_cache, value_cache, w_out,
      post_gain.reshape(1, d))


def solution(mesh):
    return jax.shard_map(
        functools.partial(shards, mesh.shape["seq"], mesh.shape["tp"]),
        mesh=mesh,
        in_specs=(
            P("seq", None),
            P(),
            P(None, "tp"),
            P("seq", "tp"),
            P("seq", "tp"),
            P("tp", None),
            P(),
            P(),
            P(),
        ),
        out_specs=P(("seq", "tp"), None),
        check_vma=False,
    )
```

profile of v0, /device:TPU:16, one launch (start us, length us, event | category | flops | bytes accessed | tf_op | source)
XLA Modules:
  0.0 122.5 jit_solution(4911321452657936071)
XLA Ops:
  0.0 1.3 %reshape.6.pre_gain = f32[1,4608]{1,0:T(1,128)} reshape(f32[4608]{0:T(1024)} %param.10) | data formatting | bytes 36864 | tf_op jit(solution)/shard_map/reshape | solution.py:424
  1.3 1.3 %reshape.7.post_gain = f32[1,4608]{1,0:T(1,128)} reshape(f32[4608]{0:T(1024)} %param.15) | data formatting | bytes 36864 | tf_op jit(solution)/shard_map/reshape | solution.py:425
  2.7 117.4 %attention_block.1 = bf16[128,4608]{1,0:T(8,128)(2,1)} custom-call(s32[8]{0:T(128)} %starts.1, s32[8]{0:T(128)} %counts.1, bf16[512,4608]{1,0:T(8,128)(2,1)} %hidden.1, f32[1,4608]{1,0:T(1,128)} %reshape.6.pre_gain, bf16[4608,1024]{1,0:T(8,128)(2,1)} %wq.1, bf16[1024,512]{1,0:T(8,128)(2,1)} %key.1, bf16[1024,512]{1,0:T(8,128)(2,1)} %value.1, ...), custom_call_target="tpu_custom_call" | custom-call | tf_op jit(solution)/shard_map/attention_block/pallas_call | solution.py:394
  120.1 2.4 %copy.11 = bf16[128,4608]{1,0:T(8,128)(2,1)} copy(bf16[128,4608]{1,0:T(8,128)(2,1)} %attention_block.1) | data formatting | bytes 2359296
where the time goes:
time: 124 us; the launch traced here: 122 us
  Pallas kernels  117 us (94%)
  local copies, waits for them, and re-layouts  5.04 us (4%)
    pallas_call x1, Pallas kernels, shards(): pl.pallas_call(functools.partial(kernel, n, n_tp, kvh), out_shape=jax.Sha...  117 us

commit v1 on v0

--- a/solution.py
+++ b/solution.py
@@ -11,9 +11,9 @@
 HEADS = 32
 HD = 128
 WINDOW = 4096
-NC = 4
+SUB = 32
 QT = 256
-NT = 512
+NT = 256
 SOFT = 50.0
 GAIN = SOFT * math.log2(math.e)
 MESH = pl.DeviceIdType.MESH
@@ -22,12 +22,13 @@
 
 
 def kernel(
-    n, n_tp, kvh,
+    n, n_tp, kvh, NC,
     starts, counts, hidden, pre_gain, wq, key, value, wout, post_gain, out,
-    hbuf, wqb, wob, k0, v0, k2, v2, k1, v1, qo, qr, vx, ao, ar, psend, precv,
-    proj, rrecv, res, obuf, att,
+    hbuf, wqb, wob, k0, v0, k2, v2, k1, v1, qo, qr, vx0, vx1, vx2, ao, ar, psend, precv,
+    proj, ra1, pa, ra2, rb1, pb, rb2, res, obuf, att,
     hsem, wqsem, wosem, kvsem, ressem, osem,
-    s2, r2, s1, r1, sq, rq, sp, rp, ss, rs,
+    s2, r2, s1, r1, sq, rq, sp, rp,
+    sa1, ta1, sa2, ta2, sb1, tb1, sb2, tb2,
 ):
     s = lax.axis_index("seq")
     t = lax.axis_index("tp")
@@ -108,11 +109,45 @@
             psend.at[c], precv.at[c], sp.at[c], rp.at[c],
             device_id=(s + 2, t), device_id_type=MESH)
 
-    def scatter(c, k):
-        to = lax.rem(t + k, n_tp)
+    nx = 2
+    ny = n_tp // nx
+    half = d // 2
+    x_own = lax.rem(t, nx)
+    y_own = lax.div(t, nx)
+    left = pl.ds(0, half)
+    right = pl.ds(half, half)
+
+    def remote(src, dst, send, recv, to):
         return pltpu.make_async_remote_copy(
-            proj.at[c, to], rrecv.at[c, k - 1], ss.at[c, k - 1], rs.at[c, k - 1],
-            device_id=(s, to), device_id_type=MESH)
+            src, dst, send, recv, device_id=(s, to), device_id_type=MESH)
+
+    def first_phase(c):
+        copies = []
+        for k in range(1, nx):
+            xt = lax.rem(x_own + k, nx)
+            copies.append(remote(
+                proj.at[c, :, xt, :, left], ra1.at[c, k - 1], sa1.at[c, k - 1], ta1.at[c, k - 1],
+                y_own * nx + xt))
+        for k in range(1, ny):
+            yt = lax.rem(y_own + k, ny)
+            copies.append(remote(
+                proj.at[c, yt, :, :, right], rb1.at[c, k - 1], sb1.at[c, k - 1], tb1.at[c, k - 1],
+                yt * nx + x_own))
+        return copies
+
+    def second_phase(c):
+        copies = []
+        for k in range(1, ny):
+            yt = lax.rem(y_own + k, ny)
+            copies.append(remote(
+                pa.at[c, yt], ra2.at[c, k - 1], sa2.at[c, k - 1], ta2.at[c, k - 1],
+                yt * nx + x_own))
+        for k in range(1, nx):
+            xt = lax.rem(x_own + k, nx)
+            copies.append(remote(
+                pb.at[c, xt], rb2.at[c, k - 1], sb2.at[c, k - 1], tb2.at[c, k - 1],
+                y_own * nx + xt))
+        return copies
 
     @pl.when(has_next)
     def _():
@@ -170,13 +205,13 @@
 
     lax.fori_loop(0, kvh, project, 0)
 
-    def extend(v, h, filled):
+    def extend(vx, v, h, filled):
         r = lax.broadcasted_iota(jnp.int32, (ctx, HD), 0)
         ok = r < filled
         vx[:, 0:HD] = jnp.where(ok, v[h].astype(F32), 0.0).astype(BF16)
         vx[:, HD:] = jnp.where(ok, 1.0, 0.0).astype(BF16)
 
-    def unit(q, k, h, acc, first, mode, offset):
+    def unit(q, k, vx, h, acc, first, mode, offset):
         per = QT // chunk
 
         def tile(i, carry):
@@ -218,17 +253,13 @@
     fill1 = counts[jnp.maximum(s - 1, 0)]
     fill2 = counts[jnp.maximum(s - 2, 0)]
 
-    def own(h, carry):
+    def own(h):
         for cp in kv_local(h):
             cp.wait()
-        extend(v0, h, ctx)
-        unit(qo, k0, h, ao, True, 1, off_own)
-        ar[h] = jnp.zeros_like(ar[h])
-        return carry
-
-    lax.fori_loop(0, kvh, own, 0)
-
-    def far(h, carry):
+        extend(vx0, v0, h, ctx)
+        unit(qo, k0, vx0, h, ao, True, 1, off_own)
+
+    def back(h):
         @pl.when(has_prev)
         def _():
             for cp in kv_next(h):
@@ -242,33 +273,49 @@
         @pl.when(has_next)
         def _():
             q_back(h).wait_recv()
+            ar[h] = jnp.zeros_like(ar[h])
 
         @pl.when(has_prev)
         def _():
-            extend(v2, h, fill2)
-            unit(qo, k2, h, ao, False, 0, 0)
+            extend(vx2, v2, h, fill2)
 
             @pl.when(has_next)
             def _():
-                unit(qr, k2, h, ar, False, 2, off_next)
+                unit(qr, k2, vx2, h, ar, False, 2, off_next)
 
         @pl.when(s >= 1)
         def _():
-            @pl.when(has_prev | (odd == 1))
-            def _():
-                for cp in kv_own_partner(h):
-                    cp.wait_recv()
-
-            extend(v1, h, fill1)
-            unit(qo, k1, h, ao, False, 0, 0)
+            for cp in kv_own_partner(h):
+                cp.wait_recv()
+
+            extend(vx1, v1, h, fill1)
 
             @pl.when(has_next)
             def _():
-                unit(qr, k1, h, ar, False, 0, 0)
-
-        return carry
-
-    lax.fori_loop(0, kvh, far, 0)
+                unit(qr, k1, vx1, h, ar, False, 0, 0)
+
+    def far(h):
+        @pl.when(has_prev)
+        def _():
+            unit(qo, k2, vx2, h, ao, False, 0, 0)
+
+        @pl.when(s >= 1)
+        def _():
+            unit(qo, k1, vx1, h, ao, False, 0, 0)
+
+    own(0)
+
+    def head(h, carry):
+        back(h)
+
+        @pl.when(h < kvh - 1)
+        def _():
+            far(h)
+            own(h + 1)
+
+        return carry
+
+    lax.fori_loop(0, kvh, head, 0)
 
     lane = lax.broadcasted_iota(jnp.int32, (chunk, HD), 1)
     heads = 2 * kvh
@@ -289,6 +336,7 @@
             psend[c, heads] = pack.astype(BF16)
             part_next(c).start()
 
+    far(kvh - 1)
     wo_copy.wait()
 
     @pl.when(s < 2)
@@ -315,15 +363,37 @@
         def column(i, inner):
             cs = pl.ds(pl.multiple_of(i * NT, NT), NT)
             y = jnp.dot(att[...], wob[:, cs], preferred_element_type=F32).astype(BF16)
-            proj[c, :, :, cs] = y.reshape(n_tp, sub, NT)
+            proj[c, :, :, :, cs] = y.reshape(ny, nx, sub, NT)
             return inner
 
         lax.fori_loop(0, d // NT, column, 0)
-        for k in range(1, n_tp):
-            scatter(c, k).start()
-        return carry
+        for cp in first_phase(c):
+            cp.start()
+
+        @pl.when(c >= 1)
+        def _():
+            middle(c - 1)
+
+        return carry
+
+    def middle(c):
+        for cp in first_phase(c):
+            cp.wait_recv()
+        for y in range(ny):
+            part = proj[c, y, x_own, :, 0:half].astype(F32)
+            for k in range(1, nx):
+                part += ra1[c, k - 1, y].astype(F32)
+            pa[c, y] = part.astype(BF16)
+        for x in range(nx):
+            part = proj[c, y_own, x, :, half:d].astype(F32)
+            for k in range(1, ny):
+                part += rb1[c, k - 1, x].astype(F32)
+            pb[c, x] = part.astype(BF16)
+        for cp in second_phase(c):
+            cp.start()
 
     lax.fori_loop(0, NC, finish, 0)
+    middle(NC - 1)
     res_copy.wait()
 
     def out_copy(c):
@@ -331,13 +401,20 @@
             obuf.at[c], out.at[pl.ds(pl.multiple_of(c * sub, sub), sub)], osem.at[c])
 
     def close(c, carry):
-        total = proj[c, t].astype(F32)
-        for k in range(1, n_tp):
-            scatter(c, k).wait_recv()
-            total += rrecv[c, k - 1].astype(F32)
-        scale = lax.rsqrt(jnp.mean(total * total, axis=-1, keepdims=True) + 0.1)
-        r = res[pl.ds(pl.multiple_of(c * sub, sub), sub)].astype(F32)
-        obuf[c] = (r + total * scale * post_gain[...]).astype(BF16)
+        for cp in second_phase(c):
+            cp.wait_recv()
+        lo = pa[c, y_own].astype(F32)
+        for k in range(1, ny):
+            lo += ra2[c, k - 1].astype(F32)
+        hi = pb[c, x_own].astype(F32)
+        for k in range(1, nx):
+            hi += rb2[c, k - 1].astype(F32)
+        squares = jnp.sum(lo * lo, axis=-1, keepdims=True) + jnp.sum(hi * hi, axis=-1, keepdims=True)
+        scale = lax.rsqrt(squares / d + 0.1)
+        span = pl.ds(pl.multiple_of(c * sub, sub), sub)
+        for v, at in ((lo, slice(0, half)), (hi, slice(half, d))):
+            r = res[span, at].astype(F32)
+            obuf[c, :, at] = (r + v * scale * post_gain[:, at]).astype(BF16)
         out_copy(c).start()
         return carry
 
@@ -372,8 +449,8 @@
         def _():
             part_next(c).wait_send()
 
-        for k in range(1, n_tp):
-            scatter(c, k).wait_send()
+        for cp in first_phase(c) + second_phase(c):
+            cp.wait_send()
         out_copy(c).wait()
         return carry
 
@@ -384,15 +461,17 @@
     rows, d = hidden_in.shape
     ctx, kvw = key_cache.shape
     kvh = kvw // HD
-    sub = rows // (NC * n_tp)
+    sub = SUB
+    NC = rows // (n_tp * sub)
     chunk = rows // NC
+    nx, ny, half = 2, n_tp // 2, d // 2
     dma = pltpu.SemaphoreType.DMA
     kv = pltpu.VMEM((kvh, ctx, HD), BF16)
     any_spec = pl.BlockSpec(memory_space=pl.ANY)
     vmem_spec = pl.BlockSpec(memory_space=pltpu.VMEM)
     smem_spec = pl.BlockSpec(memory_space=pltpu.SMEM)
     return pl.pallas_call(
-        functools.partial(kernel, n, n_tp, kvh),
+        functools.partial(kernel, n, n_tp, kvh, NC),
         out_shape=jax.ShapeDtypeStruct((rows // n_tp, d), BF16),
         in_specs=[smem_spec, smem_spec, any_spec, vmem_spec] + [any_spec] * 4 + [vmem_spec],
         out_specs=any_spec,
@@ -404,19 +483,27 @@
             pltpu.VMEM((kvh, 2 * rows, HD), BF16),
             pltpu.VMEM((kvh, 2 * rows, HD), BF16),
             pltpu.VMEM((ctx, 2 * HD), BF16),
+            pltpu.VMEM((ctx, 2 * HD), BF16),
+            pltpu.VMEM((ctx, 2 * HD), BF16),
             pltpu.VMEM((kvh, 2 * rows, 2 * HD), F32),
             pltpu.VMEM((kvh, 2 * rows, 2 * HD), F32),
             pltpu.VMEM((NC, 2 * kvh + 1, chunk, HD), BF16),
             pltpu.VMEM((NC, 2 * kvh + 1, chunk, HD), BF16),
-            pltpu.VMEM((NC, n_tp, sub, d), BF16),
-            pltpu.VMEM((NC, n_tp - 1, sub, d), BF16),
+            pltpu.VMEM((NC, ny, nx, sub, d), BF16),
+            pltpu.VMEM((NC, nx - 1, ny, sub, half), BF16),
+            pltpu.VMEM((NC, ny, sub, half), BF16),
+            pltpu.VMEM((NC, ny - 1, sub, half), BF16),
+            pltpu.VMEM((NC, ny - 1, nx, sub, half), BF16),
+            pltpu.VMEM((NC, nx, sub, half), BF16),
+            pltpu.VMEM((NC, nx - 1, sub, half), BF16),
             pltpu.VMEM((rows // n_tp, d), BF16),
             pltpu.VMEM((NC, sub, d), BF16),
             pltpu.VMEM((chunk, w_out.shape[0]), BF16),
             dma((NC, n_tp)), dma((kvh,)), dma, dma((kvh, 2)), dma, dma((NC,)),
             dma((kvh, 2)), dma((kvh, 2)), dma((kvh, 2)), dma((kvh, 2)),
             dma((kvh,)), dma((kvh,)), dma((NC,)), dma((NC,)),
-            dma((NC, n_tp - 1)), dma((NC, n_tp - 1)),
+            dma((NC, nx - 1)), dma((NC, nx - 1)), dma((NC, ny - 1)), dma((NC, ny - 1)),
+            dma((NC, ny - 1)), dma((NC, ny - 1)), dma((NC, nx - 1)), dma((NC, nx - 1)),
         ],
         compiler_params=pltpu.CompilerParams(
             collective_id=0, has_side_effects=True, vmem_limit_bytes=67_000_000),

time: 124 us -> 113 us (0.911)
  Pallas kernels: 117 us -> 108 us
    pallas_call x1, Pallas kernels: 117 us -> 108 us  [shards(): pl.pallas_call(functools.partial(kernel, n, n_tp, kvh, NC), out_shape=jax...]
where the time goes in v1:
time: 113 us
  Pallas kernels  108 us (96%)
  local copies, waits for them, and re-layouts  5.04 us (4%)
    pallas_call x1, Pallas kernels, shards(): pl.pallas_call(functools.partial(kernel, n, n_tp, kvh, NC), out_shape=jax...  108 us
    unnamed x1, local copies, waits for them, and re-layouts  2.36 us

profile of v1, /device:TPU:16, one launch (start us, length us, event | category | flops | bytes accessed | tf_op | source)
XLA Modules:
  0.0 112.6 jit_solution(15407870605028782225)
XLA Ops:
  0.0 1.3 %reshape.6.pre_gain = f32[1,4608]{1,0:T(1,128)} reshape(f32[4608]{0:T(1024)} %param.10) | data formatting | bytes 36864 | tf_op jit(solution)/shard_map/reshape | solution.py:511
  1.3 1.3 %reshape.7.post_gain = f32[1,4608]{1,0:T(1,128)} reshape(f32[4608]{0:T(1024)} %param.15) | data formatting | bytes 36864 | tf_op jit(solution)/shard_map/reshape | solution.py:512
  2.7 107.5 %attention_block.1 = bf16[128,4608]{1,0:T(8,128)(2,1)} custom-call(s32[8]{0:T(128)} %starts.1, s32[8]{0:T(128)} %counts.1, bf16[512,4608]{1,0:T(8,128)(2,1)} %hidden.1, f32[1,4608]{1,0:T(1,128)} %reshape.6.pre_gain, bf16[4608,1024]{1,0:T(8,128)(2,1)} %wq.1, bf16[1024,512]{1,0:T(8,128)(2,1)} %key.1, bf16[1024,512]{1,0:T(8,128)(2,1)} %value.1, ...), custom_call_target="tpu_custom_call" | custom-call | tf_op jit(solution)/shard_map/attention_block/pallas_call | solution.py:473
  110.2 2.4 %copy.11 = bf16[128,4608]{1,0:T(8,128)(2,1)} copy(bf16[128,4608]{1,0:T(8,128)(2,1)} %attention_block.1) | data formatting | bytes 2359296

commit v2 on v1

--- a/solution.py
+++ b/solution.py
@@ -11,7 +11,7 @@
 HEADS = 32
 HD = 128
 WINDOW = 4096
-SUB = 32
+SUB = 16
 QT = 256
 NT = 256
 SOFT = 50.0

time: 113 us -> 112 us (level)
  no operation moved by 1% of the time
where the time goes in v2:
time: 112 us
  Pallas kernels  107 us (96%)
  local copies, waits for them, and re-layouts  5.04 us (4%)
    pallas_call x1, Pallas kernels, shards(): pl.pallas_call(functools.partial(kernel, n, n_tp, kvh, NC), out_shape=jax...  107 us
    unnamed x1, local copies, waits for them, and re-layouts  2.36 us

profile of v2, /device:TPU:16, one launch (start us, length us, event | category | flops | bytes accessed | tf_op | source)
XLA Modules:
  0.0 112.1 jit_solution(13422266192498942079)
XLA Ops:
  0.0 1.3 %reshape.6.pre_gain = f32[1,4608]{1,0:T(1,128)} reshape(f32[4608]{0:T(1024)} %param.10) | data formatting | bytes 36864 | tf_op jit(solution)/shard_map/reshape | solution.py:511
  1.3 1.3 %reshape.7.post_gain = f32[1,4608]{1,0:T(1,128)} reshape(f32[4608]{0:T(1024)} %param.15) | data formatting | bytes 36864 | tf_op jit(solution)/shard_map/reshape | solution.py:512
  2.7 107.0 %attention_block.1 = bf16[128,4608]{1,0:T(8,128)(2,1)} custom-call(s32[8]{0:T(128)} %starts.1, s32[8]{0:T(128)} %counts.1, bf16[512,4608]{1,0:T(8,128)(2,1)} %hidden.1, f32[1,4608]{1,0:T(1,128)} %reshape.6.pre_gain, bf16[4608,1024]{1,0:T(8,128)(2,1)} %wq.1, bf16[1024,512]{1,0:T(8,128)(2,1)} %key.1, bf16[1024,512]{1,0:T(8,128)(2,1)} %value.1, ...), custom_call_target="tpu_custom_call" | custom-call | tf_op jit(solution)/shard_map/attention_block/pallas_call | solution.py:473
  109.7 2.4 %copy.11 = bf16[128,4608]{1,0:T(8,128)(2,1)} copy(bf16[128,4608]{1,0:T(8,128)(2,1)} %attention_block.1) | data formatting | bytes 2359296
